TPU v7x, 32 devices: a whole 2x2x4 slice. The times are simulated.
32 devices in a mesh: dp: 8 (over y, x, core), seq: 4 (over z).
Axes of the slice: x: 2, y: 2, z: 4, core: 2. Of those that a mesh axis runs over, the one named last changes fastest.
Arguments:
- student_in: bfloat16 [4096, 3584], P(('dp', 'seq')), may hold values from -6 to 6
- weight: bfloat16 [3584, 512], P(('dp', 'seq')), may hold values from -0.09375 to 0.09375
- queries: bfloat16 [4096, 512], P(('dp', 'seq')), may hold values from -8 to 8, as said below
- keys: bfloat16 [4096, 128], P(('dp', 'seq')), may hold values from -8 to 8
- values: bfloat16 [4096, 128], P(('dp', 'seq')), may hold values from -6 to 6
- lengths: int32 [8, 4], P('dp'), may hold values from 1 to 384, 512 in all within a row
- assignment: int32 [8, 4], P('dp'), may hold values from 0 to 3, each once within a row
Outputs:
- attention: bfloat16 [4096, 512], P(('dp', 'seq'))
- weight_grad: float32 [3584, 512], P(('dp', 'seq'))
Inputs may be any that keep to these rules, and one draw needn't show every extreme that they name: `queries`: entries of head 0 and of keys may reach the ends of this range. Each row holds the lengths of 4 rollouts of one sequence, summing to 512, the longest exactly 384. `assignment`: each row is a permutation of the 4 rollout blocks of one sequence.
All inputs are finite; a program needn't handle non-finite values.
Results may differ from a plain program's by a relative error of at most 0.012.
Values may be sent and summed in bfloat16 or wider, within the bound.
A program may use at most 64 MiB of HBM per device.

v0:
```python
import math
import jax
import jax.numpy as jnp
from jax import lax
from jax.sharding import PartitionSpec as P

HD = 128
HQ = 4
BLK = 128
EPSILON = 1e-06
NEGATIVE = -1e30


def locate(assign_row, doc_ends, first_slot, count):
    slot_ids = first_slot + jnp.arange(count, dtype=jnp.int32)
    block_ids = slot_ids // BLK
    block_table = jnp.arange(assign_row.shape[0], dtype=jnp.int32)
    placed = jnp.sum(
        jnp.where(block_ids[:, None] == block_table[None, :], assign_row[None, :], 0), axis=1
    )
    position = placed * BLK + slot_ids % BLK
    document = jnp.sum((position[:, None] >= doc_ends[None, :]).astype(jnp.int32), axis=1)
    return (position, document)


def absorb_block(state, key_block, value_block, query_heads, allowed):
    run_max, run_total, run_acc = state
    scores = jnp.einsum(
        "qhd,kd->hqk", query_heads, key_block, preferred_element_type=jnp.float32
    ) * HD ** (-0.5)
    masked = jnp.where(allowed[None], scores, NEGATIVE)
    new_max = jnp.maximum(run_max, jnp.max(masked, axis=-1))
    fading = jnp.exp(run_max - new_max)
    exp_terms = jnp.where(allowed[None], jnp.exp(masked - new_max[:, :, None]), 0.0)
    new_total = run_total * fading + jnp.sum(exp_terms, axis=-1)
    mixture = jnp.einsum(
        "hqk,kd->qhd",
        exp_terms.astype(jnp.bfloat16),
        value_block,
        preferred_element_type=jnp.float32,
    )
    new_acc = run_acc * fading.T[:, :, None] + mixture
    return (new_max, new_total, new_acc)


def local(student_in, weight, queries, keys, values, lengths, assignment):
    rows = queries.shape[0]
    assign_row = assignment[0]
    doc_ends = jnp.cumsum(lengths[0])
    query_pos, query_doc = locate(assign_row, doc_ends, lax.axis_index("seq") * rows, rows)
    query_heads = queries.reshape(rows, HQ, HD)
    start_state = (
        jnp.full((HQ, rows), NEGATIVE, jnp.float32),
        jnp.zeros((HQ, rows), jnp.float32),
        jnp.zeros((rows, HQ, HD), jnp.float32),
    )
    key_piece = lax.all_gather(keys, "seq", axis=0, tiled=True)
    value_piece = lax.all_gather(values, "seq", axis=0, tiled=True)
    count = key_piece.shape[0]
    step_rows = math.gcd(count, 512)
    steps_count = count // step_rows
    key_pos, key_doc = locate(assign_row, doc_ends, jnp.int32(0), count)

    def one_step(running, slabs):
        key_block, value_block, key_position, key_document = slabs
        allowed = (query_doc[:, None] == key_document[None, :]) & (
            query_pos[:, None] >= key_position[None, :]
        )
        updated = absorb_block(running, key_block, value_block, query_heads, allowed)
        return (updated, None)

    slabs = (
        key_piece.reshape(steps_count, step_rows, HD),
        value_piece.reshape(steps_count, step_rows, HD),
        key_pos.reshape(steps_count, step_rows),
        key_doc.reshape(steps_count, step_rows),
    )
    result, _ = lax.scan(one_step, start_state, slabs)
    final_max, final_total, final_acc = result
    attention = (final_acc / final_total.T[:, :, None]).reshape(rows, HQ * HD).astype(jnp.bfloat16)
    as_float = student_in.astype(jnp.float32)
    normed = (
        as_float * lax.rsqrt(jnp.mean(as_float * as_float, axis=1, keepdims=True) + EPSILON)
    ).astype(jnp.bfloat16)
    group_rows = lax.all_gather(weight, "seq", axis=0, tiled=True)
    columns = normed
    predicted = jnp.dot(
        columns,
        lax.all_gather(group_rows, "dp", axis=0, tiled=True),
        preferred_element_type=jnp.float32,
    )
    dp_count = lax.axis_size("dp")
    seq_count = lax.axis_size("seq")
    token_total = rows * dp_count * seq_count
    scaled = ((predicted - attention.astype(jnp.float32)) * token_total ** (-0.5)).astype(
        jnp.bfloat16
    )
    columns = normed
    outer_rows = lax.psum_scatter(
        lax.dot_general(
            columns, scaled, (((0,), (0,)), ((), ())), preferred_element_type=jnp.float32
        ).astype(jnp.bfloat16),
        "dp",
        scatter_dimension=0,
        tiled=True,
    )
    weight_grad = lax.psum_scatter(outer_rows, "seq", scatter_dimension=0, tiled=True).astype(
        jnp.float32
    )
    return (attention, weight_grad)


def solution(mesh):
    placed = (
        P(("dp", "seq"), None),
        P(("dp", "seq"), None),
        P(("dp", "seq"), None),
        P(("dp", "seq"), None),
        P(("dp", "seq"), None),
        P("dp", None),
        P("dp", None),
    )
    return jax.shard_map(
        local,
        mesh=mesh,
        in_specs=placed,
        out_specs=(P(("dp", "seq"), None), P(("dp", "seq"), None)),
        check_vma=False,
    )
```

profile of v0, /device:TPU:0, one launch (start us, length us, event | category | flops | bytes accessed | tf_op | source)
XLA Modules:
  0.0 149.0 jit_solution(12489444883028070864)
XLA Ops:
  7.2 0.0 copy-start
  7.2 0.0 copy-start.1
  7.2 0.0 all-gather.2.cloned.1.call-start
  7.2 18.8 %all_gather.14 = bf16[448,512]{1,0:T(8,128)(2,1)} all-gather(bf16[112,512]{1,0:T(8,128)(2,1)} %param.8), channel_id=1, replica_groups=mesh['dp'=8,'seq'=4] {'seq'}, dimensions={0}, use_global_device_ids=true | all-gather | bytes 573440 | tf_op jit(solution)/shard_map/all_gather | solution.py:85
  26.0 0.0 all-gather.2.cloned.1.call-update
  26.0 0.0 reduce-scatter.3.cloned.1.call-start
  26.1 0.9 copy.14
  26.9 0.8 reduce-window.8
  27.8 12.3 %all_gather.13 = bf16[512,128]{0,1:T(8,128)(2,1)S(1)} all-gather(bf16[128,128]{0,1:T(8,128)(2,1)S(1)} %copy.14), channel_id=1, replica_groups=mesh['dp'=8,'seq'=4] {'seq'}, dimensions={0}, use_global_device_ids=true | all-gather | bytes 163840 | tf_op jit(solution)/shard_map/all_gather | solution.py:58
  40.1 13.5 %all_gather.12 = bf16[512,128]{1,0:T(8,128)(2,1)S(1)} all-gather(bf16[128,128]{1,0:T(8,128)(2,1)} %param.10), channel_id=1, replica_groups=mesh['dp'=8,'seq'=4] {'seq'}, dimensions={0}, use_global_device_ids=true | all-gather | bytes 163840 | tf_op jit(solution)/shard_map/all_gather | solution.py:57
  53.7 0.7 select_reduce_fusion.1
  54.5 0.1 convert_reduce_fusion.1
  54.5 0.7 select_reduce_fusion
  55.3 0.1 convert_reduce_fusion
  55.4 1.4 fusion
  56.8 0.2 compare_and_fusion
  57.0 0.0 copy-done
  57.1 0.3 fusion.36
  57.4 0.2 fusion.13
  57.6 0.3 fusion.8
  58.0 2.6 %all-gather.2.cloned.1.call-done = bf16[3584,512]{1,0:T(8,128)(2,1)} async-done(((bf16[448,512]{1,0:T(8,128)(2,1)}), bf16[3584,512]{1,0:T(8,128)(2,1)}) %all-gather.2.cloned.1.call-update) | async-done | bytes 3670032 | tf_op jit(solution)/shard_map/all_gather | solution.py:89
  60.6 0.0 copy-done.1
  60.6 7.9 %convolution_convert_fusion = bf16[3584,512]{1,0:T(8,128)(2,1)} fusion(bf16[3584,512]{1,0:T(8,128)(2,1)} %all-gather.2.cloned.1.call-done, bf16[128,3584]{1,0:T(8,128)(2,1)S(1)} %copy-done.1, f32[128]{0:T(128)S(1)} %add_rsqrt_fusion, bf16[128,512]{0,1:T(8,128)(2,1)S(1)} %bitcast.40), kind=kOutput, calls=%fused_computation | convolution fusion | flops 944373760 | bytes 8389120 | tf_op jit(solution)/shard_map/dot_general | solution.py:100
  68.5 0.0 reduce-scatter.3.cloned.1.call-update
  68.6 0.0 reduce-scatter.5.cloned.1.call-start
  68.6 48.7 %reduce-scatter.3.cloned.1.call-done = bf16[448,512]{1,0:T(8,128)(2,1)} async-done(((bf16[3584,512]{1,0:T(8,128)(2,1)}), bf16[448,512]{1,0:T(8,128)(2,1)}) %reduce-scatter.3.cloned.1.call-update) | async-done | bytes 458768 | tf_op jit(solution)/shard_map/reduce_scatter | solution.py:99
  117.3 0.0 reduce-scatter.5.cloned.1.call-update
  117.3 0.8 copy.16
  118.1 22.8 %reduce-scatter.5.cloned.1.call-done = bf16[112,512]{1,0:T(8,128)(2,1)} async-done(((bf16[448,512]{1,0:T(8,128)(2,1)}), bf16[112,512]{1,0:T(8,128)(2,1)}) %reduce-scatter.5.cloned.1.call-update) | async-done | bytes 114704 | tf_op jit(solution)/shard_map/reduce_scatter | solution.py:107
  140.9 1.6 %convert_element_type.44 = f32[112,512]{1,0:T(8,128)} convert(bf16[112,512]{1,0:T(8,128)(2,1)} %reduce-scatter.5.cloned.1.call-done) | non-fusion elementwise | flops 57344 | bytes 344064 | tf_op jit(solution)/shard_map/convert_element_type | solution.py:107
  (7 shorter events, 0.1 us)
Async XLA Ops:
  7.2 49.9 %copy-start = (bf16[128,512]{1,0:T(8,128)(2,1)S(1)}, bf16[128,512]{1,0:T(8,128)(2,1)}, u32[]{:S(2)}) copy-start(bf16[128,512]{1,0:T(8,128)(2,1)} %param.9) | copy-start | bytes 393220
  7.2 53.4 %copy-start.1 = (bf16[128,3584]{1,0:T(8,128)(2,1)S(1)}, bf16[128,3584]{1,0:T(8,128)(2,1)}, u32[]{:S(2)}) copy-start(bf16[128,3584]{1,0:T(8,128)(2,1)} %param.7) | copy-start | bytes 2752516
  7.2 53.4 %all-gather.2.cloned.1.call-start = ((), (), s32[]{:S(2)}) async-start(), calls=%async_computation.2 | async-start | bytes 4128768 | tf_op jit(solution)/shard_map/all_gather | solution.py:89
  26.0 91.3 %reduce-scatter.3.cloned.1.call-start = ((), (), s32[]{:S(2)}) async-start(), calls=%async_computation.3 | async-start | bytes 4128768 | tf_op jit(solution)/shard_map/reduce_scatter | solution.py:99
  68.6 72.3 %reduce-scatter.5.cloned.1.call-start = ((), (), s32[]{:S(2)}) async-start(), calls=%async_computation.4 | async-start | bytes 573440 | tf_op jit(solution)/shard_map/reduce_scatter | solution.py:107
Sparse Core Ops, SparseCore 0:
  26.1 34.3 all-gather.1
  68.7 48.5 reduce-scatter.2
  119.6 21.2 reduce-scatter.4
where the time goes:
time: 149 us
  waiting for transfers between devices  74.2 us (50%)
  blocking collectives  44.7 us (30%)
  between operations  13.8 us (9%)
  matrix products  8.59 us (6%)
  other arithmetic  6.01 us (4%)
  local copies, waits for them, and re-layouts  1.65 us (1%)
    reduce_scatter x1, waiting for transfers between devices, local(): lax.psum_scatter(lax.dot_general(columns, scaled, (((0,), (0,)), ((), ())...  48.7 us
    reduce_scatter x1, waiting for transfers between devices, local(): lax.psum_scatter(outer_rows, 'seq', scatter_dimension=0, tiled=True)  22.8 us
    all_gather x1, blocking collectives, local(): group_rows = lax.all_gather(weight, 'seq', axis=0, tiled=True)  18.8 us
    all_gather x1, blocking collectives, local(): key_piece = lax.all_gather(keys, 'seq', axis=0, tiled=True)  13.5 us
    all_gather x1, blocking collectives, local(): value_piece = lax.all_gather(values, 'seq', axis=0, tiled=True)  12.3 us
    dot_general x1, matrix products, local(): lax.dot_general(columns, scaled, (((0,), (0,)), ((), ())), preferred_elem...  7.94 us
  transfers between devices with their start and end apart: 3, of which 3 were waited for; matrix products, arithmetic and copies ran while one was open for 4% of the time, Pallas kernels for 0%

commit v1 on v0

--- a/solution.py
+++ b/solution.py
@@ -55,7 +55,13 @@
         jnp.zeros((rows, HQ, HD), jnp.float32),
     )
     key_piece = lax.all_gather(keys, "seq", axis=0, tiled=True)
-    value_piece = lax.all_gather(values, "seq", axis=0, tiled=True)
+    size = lax.axis_size("seq")
+    held, tiles = (values, [values])
+    for _ in range(size - 1):
+        held = lax.ppermute(held, "seq", [(i, (i + 1) % size) for i in range(size)])
+        tiles.insert(0, held)
+    row_of_blocks = jnp.concatenate(tiles, axis=0)
+    value_piece = jnp.roll(row_of_blocks, (lax.axis_index("seq") + 1) * values.shape[0], axis=0)
     count = key_piece.shape[0]
     step_rows = math.gcd(count, 512)
     steps_count = count // step_rows

time: 149 us -> 149 us (level)
  blocking collectives: 44.7 us -> 32.8 us
  waiting for transfers between devices: 74.2 us -> 85.3 us
  starting transfers between devices: 0.12 us -> 1.92 us
    all_gather x1 -> x0, blocking collectives: 12.3 us -> none  [local(): value_piece = lax.all_gather(values, 'seq', axis=0, tiled=True)]
    ppermute x0 -> x3, waiting for transfers between devices: none -> 9.88 us  [local(): held = lax.ppermute(held, 'seq', [(i, (i + 1) % size) for i in range(size)])]
    ppermute x0 -> x3, starting transfers between devices: none -> 1.8 us  [local(): held = lax.ppermute(held, 'seq', [(i, (i + 1) % size) for i in range(size)])]
  transfers between devices with their start and end apart: 3 -> 6, of which waited for: 3 -> 5; matrix products, arithmetic and copies ran while one was open for 4% -> 4% of each run, Pallas kernels for 0% -> 0%
where the time goes in v1:
time: 149 us
  waiting for transfers between devices  85.3 us (57%)
  blocking collectives  32.8 us (22%)
  between operations  13.9 us (9%)
  matrix products  8.58 us (6%)
  other arithmetic  4.83 us (3%)
  starting transfers between devices  1.92 us (1%)
  local copies, waits for them, and re-layouts  1.75 us (1%)
    reduce_scatter x1, waiting for transfers between devices, local(): lax.psum_scatter(lax.dot_general(columns, scaled, (((0,), (0,)), ((), ())...  48.7 us
    reduce_scatter x1, waiting for transfers between devices, local(): lax.psum_scatter(outer_rows, 'seq', scatter_dimension=0, tiled=True)  22.8 us
    all_gather x1, blocking collectives, local(): group_rows = lax.all_gather(weight, 'seq', axis=0, tiled=True)  18.8 us
    all_gather x1, blocking collectives, local(): key_piece = lax.all_gather(keys, 'seq', axis=0, tiled=True)  14 us
    ppermute x3, waiting for transfers between devices, local(): held = lax.ppermute(held, 'seq', [(i, (i + 1) % size) for i in range(size)])  9.88 us
    dot_general x1, matrix products, local(): lax.dot_general(columns, scaled, (((0,), (0,)), ((), ())), preferred_elem...  7.94 us
    all_gather x1, waiting for transfers between devices, local(): lax.all_gather(group_rows, 'dp', axis=0, tiled=True)  3.91 us
  transfers between devices with their start and end apart: 6, of which 5 were waited for; matrix products, arithmetic and copies ran while one was open for 4% of the time, Pallas kernels for 0%

profile of v1, /device:TPU:0, one launch (start us, length us, event | category | flops | bytes accessed | tf_op | source)
XLA Modules:
  0.0 149.0 jit_solution(4657982836793132429)
XLA Ops:
  7.2 0.0 copy-start
  7.2 0.0 copy-start.1
  7.2 0.0 all-gather.2.cloned.1.call-start
  7.2 18.8 %all_gather.10 = bf16[448,512]{1,0:T(8,128)(2,1)} all-gather(bf16[112,512]{1,0:T(8,128)(2,1)} %param.8), channel_id=1, replica_groups=mesh['dp'=8,'seq'=4] {'seq'}, dimensions={0}, use_global_device_ids=true | all-gather | bytes 573440 | tf_op jit(solution)/shard_map/all_gather | solution.py:91
  26.0 0.0 all-gather.2.cloned.1.call-update
  26.0 0.0 reduce-scatter.3.cloned.1.call-start
  26.1 0.9 copy.16
  26.9 0.5 collective-permute-start
  27.4 0.8 reduce-window.8
  28.2 14.0 %all_gather.9 = bf16[512,128]{1,0:T(8,128)(2,1)S(1)} all-gather(bf16[128,128]{1,0:T(8,128)(2,1)} %param.10), channel_id=1, replica_groups=mesh['dp'=8,'seq'=4] {'seq'}, dimensions={0}, use_global_device_ids=true | all-gather | bytes 163840 | tf_op jit(solution)/shard_map/all_gather | solution.py:57
  42.3 0.7 select_reduce_fusion.1
  43.0 0.1 convert_reduce_fusion.1
  43.1 0.7 select_reduce_fusion
  43.9 0.1 convert_reduce_fusion
  43.9 0.2 compare_and_fusion
  44.2 0.0 copy-done
  44.2 0.3 fusion.38
  44.5 0.2 fusion.13
  44.7 0.0 collective-permute-done
  44.7 1.3 collective-permute-start.1
  46.1 0.0 copy-done.1
  46.1 0.3 fusion
  46.3 4.2 %collective-permute-done.1 = bf16[128,128]{0,1:T(8,128)(2,1)S(1)} collective-permute-done((bf16[128,128]{0,1:T(8,128)(2,1)S(1)}, bf16[128,128]{0,1:T(8,128)(2,1)S(1)}, u32[]{:S(2)}, u32[]{:S(2)}) %collective-permute-start.1) | collective-permute-done | bytes 32800 | tf_op jit(solution)/shard_map/ppermute | solution.py:61
  50.5 0.0 collective-permute-start.2
  50.5 5.7 %collective-permute-done.2 = bf16[128,128]{0,1:T(8,128)(2,1)S(1)} collective-permute-done((bf16[128,128]{0,1:T(8,128)(2,1)S(1)}, bf16[128,128]{0,1:T(8,128)(2,1)S(1)}, u32[]{:S(2)}, u32[]{:S(2)}) %collective-permute-start.2) | collective-permute-done | bytes 32800 | tf_op jit(solution)/shard_map/ppermute | solution.py:61
  56.3 0.3 fusion.8
  56.7 3.9 %all-gather.2.cloned.1.call-done = bf16[3584,512]{1,0:T(8,128)(2,1)} async-done(((bf16[448,512]{1,0:T(8,128)(2,1)}), bf16[3584,512]{1,0:T(8,128)(2,1)}) %all-gather.2.cloned.1.call-update) | async-done | bytes 3670032 | tf_op jit(solution)/shard_map/all_gather | solution.py:95
  60.6 7.9 %convolution_convert_fusion = bf16[3584,512]{1,0:T(8,128)(2,1)} fusion(bf16[3584,512]{1,0:T(8,128)(2,1)} %all-gather.2.cloned.1.call-done, bf16[128,3584]{1,0:T(8,128)(2,1)S(1)} %copy-done.1, f32[128]{0:T(128)S(1)} %add_rsqrt_fusion, bf16[128,512]{0,1:T(8,128)(2,1)S(1)} %bitcast.40), kind=kOutput, calls=%fused_computation | convolution fusion | flops 944373760 | bytes 8389120 | tf_op jit(solution)/shard_map/dot_general | solution.py:106
  68.5 0.0 reduce-scatter.3.cloned.1.call-update
  68.6 0.0 reduce-scatter.5.cloned.1.call-start
  68.6 48.7 %reduce-scatter.3.cloned.1.call-done = bf16[448,512]{1,0:T(8,128)(2,1)} async-done(((bf16[3584,512]{1,0:T(8,128)(2,1)}), bf16[448,512]{1,0:T(8,128)(2,1)}) %reduce-scatter.3.cloned.1.call-update) | async-done | bytes 458768 | tf_op jit(solution)/shard_map/reduce_scatter | solution.py:105
  117.3 0.0 reduce-scatter.5.cloned.1.call-update
  117.3 0.8 copy.20
  118.1 22.8 %reduce-scatter.5.cloned.1.call-done = bf16[112,512]{1,0:T(8,128)(2,1)} async-done(((bf16[448,512]{1,0:T(8,128)(2,1)}), bf16[112,512]{1,0:T(8,128)(2,1)}) %reduce-scatter.5.cloned.1.call-update) | async-done | bytes 114704 | tf_op jit(solution)/shard_map/reduce_scatter | solution.py:113
  140.9 1.6 %convert_element_type.44 = f32[112,512]{1,0:T(8,128)} convert(bf16[112,512]{1,0:T(8,128)(2,1)} %reduce-scatter.5.cloned.1.call-done) | non-fusion elementwise | flops 57344 | bytes 344064 | tf_op jit(solution)/shard_map/convert_element_type | solution.py:113
  (15 shorter events, 0.2 us)
Async XLA Ops:
  7.2 37.0 %copy-start = (bf16[128,512]{1,0:T(8,128)(2,1)S(1)}, bf16[128,512]{1,0:T(8,128)(2,1)}, u32[]{:S(2)}) copy-start(bf16[128,512]{1,0:T(8,128)(2,1)} %param.9) | copy-start | bytes 393220
  7.2 38.9 %copy-start.1 = (bf16[128,3584]{1,0:T(8,128)(2,1)S(1)}, bf16[128,3584]{1,0:T(8,128)(2,1)}, u32[]{:S(2)}) copy-start(bf16[128,3584]{1,0:T(8,128)(2,1)} %param.7) | copy-start | bytes 2752516
  7.2 53.4 %all-gather.2.cloned.1.call-start = ((), (), s32[]{:S(2)}) async-start(), calls=%async_computation.2 | async-start | bytes 4128768 | tf_op jit(solution)/shard_map/all_gather | solution.py:95
  26.0 91.2 %reduce-scatter.3.cloned.1.call-start = ((), (), s32[]{:S(2)}) async-start(), calls=%async_computation.3 | async-start | bytes 4128768 | tf_op jit(solution)/shard_map/reduce_scatter | solution.py:105
  26.9 17.8 %collective-permute-start = (bf16[128,128]{0,1:T(8,128)(2,1)S(1)}, bf16[128,128]{0,1:T(8,128)(2,1)S(1)}, u32[]{:S(2)}, u32[]{:S(2)}) collective-permute-start(bf16[128,128]{0,1:T(8,128)(2,1)S(1)} %copy.16), channel_id=1, source_target_pairs={{0,1},{1,2},{2,3},{3,0},{4,5},{5,6},{6,7},{7,4},{8,9},{9,10},{10,1... | collective-permute-start | bytes 98312 | tf_op jit(solution)/shard_map/ppermute | solution.py:61
  44.7 5.8 %collective-permute-start.1 = (bf16[128,128]{0,1:T(8,128)(2,1)S(1)}, bf16[128,128]{0,1:T(8,128)(2,1)S(1)}, u32[]{:S(2)}, u32[]{:S(2)}) collective-permute-start(bf16[128,128]{0,1:T(8,128)(2,1)S(1)} %collective-permute-done), channel_id=1, source_target_pairs={{0,1},{1,2},{2,3},{3,0},{4,5},{5,6},{6,7},{7,4},{8,9},{9,10},{10,1... | collective-permute-start | bytes 98312 | tf_op jit(solution)/shard_map/ppermute | solution.py:61
  50.5 5.7 %collective-permute-start.2 = (bf16[128,128]{0,1:T(8,128)(2,1)S(1)}, bf16[128,128]{0,1:T(8,128)(2,1)S(1)}, u32[]{:S(2)}, u32[]{:S(2)}) collective-permute-start(bf16[128,128]{0,1:T(8,128)(2,1)S(1)} %collective-permute-done.1), channel_id=1, source_target_pairs={{0,1},{1,2},{2,3},{3,0},{4,5},{5,6},{6,7},{7,4},{8,9},{9,10},{10,1... | collective-permute-start | bytes 98312 | tf_op jit(solution)/shard_map/ppermute | solution.py:61
  68.6 72.3 %reduce-scatter.5.cloned.1.call-start = ((), (), s32[]{:S(2)}) async-start(), calls=%async_computation.4 | async-start | bytes 573440 | tf_op jit(solution)/shard_map/reduce_scatter | solution.py:113
Sparse Core Ops, SparseCore 0:
  26.1 34.3 all-gather.1
  68.7 48.5 reduce-scatter.2
  119.6 21.2 reduce-scatter.4
